TPU v7x, 32 devices: a whole 2x2x4 slice. The times are simulated.
32 devices in a mesh: inst: 4 (over x, core), gx: 2 (over y), gy: 4 (over z).
Axes of the slice: x: 2, y: 2, z: 4, core: 2. Of those that a mesh axis runs over, the one named last changes fastest.
Arguments:
- state: float32 [8, 5, 16, 32, 128], P('inst', None, 'gx', 'gy'), may hold values from -6 to 6
- source: float32 [8, 5, 16, 32, 128], P('inst', None, 'gx', 'gy'), may hold values from -60 to 60
- jacobian: float32 [8, 5, 5, 16, 32, 128], P('inst', None, None, 'gx', 'gy'), may hold values from -1.5 to 16, as said below
- couplings: float32 [6, 5, 5], replicated, may hold values from -0.625 to 0.625
- omega: float32 [1], replicated, may hold values from 0.2 to 0.6
Outputs:
- state_next: float32 [8, 5, 16, 32, 128], P('inst', None, 'gx', 'gy')
- last_residual: float32 [8, 5, 16, 32, 128], P('inst', None, 'gx', 'gy')
Inputs may be any that keep to these rules, and one draw needn't show every extreme that they name: In every block jacobian[n, :, :, cell] each diagonal entry lies in 8 to 16 and exceeds the sum of magnitudes of the other entries of its row by 2 or more.
All inputs are finite; a program needn't handle non-finite values.
Results may differ from a plain program's by a relative error of at most 0.0003.
Values sent between devices are 32-bit elements; how exact they have to be, the bound alone decides.
A program may use at most 64 MiB of HBM per device.

v0:
```python
import jax
import jax.numpy as jnp
from jax import lax
from jax.sharding import PartitionSpec as P

ITERS = 3


def with_halo(block, sides, width, periodic):
    for axis, dim in sides:
        count = lax.axis_size(axis)
        forward = [(i, i + 1) for i in range(count - 1)]
        if periodic:
            forward.append((count - 1, 0))
        backward = [(target, source) for source, target in forward]
        low = lax.ppermute(
            lax.slice_in_dim(block, block.shape[dim] - width, None, axis=dim), axis, forward
        )
        high = lax.ppermute(lax.slice_in_dim(block, 0, width, axis=dim), axis, backward)
        block = jnp.concatenate([low, block, high], axis=dim)
    return block


def spectral_table(row_index, column_index, total):
    offset = row_index[:, None] - column_index[None, :]
    parity = 1.0 - 2.0 * jnp.mod(offset, 2).astype(jnp.float32)
    angle = jnp.pi * offset.astype(jnp.float32) / total
    onsite = offset == 0
    sine = jnp.where(onsite, jnp.ones_like(angle), jnp.sin(angle))
    return jnp.where(onsite, jnp.zeros_like(angle), 0.5 * parity * jnp.cos(angle) / sine)


def apply_table(table, field):
    return jnp.einsum("nm,mvxyz->nvxyz", table, field, precision=lax.Precision.HIGHEST)


def neighbours(padded, couplings):
    shifted = [
        padded[:, :, :-2, 1:-1, 1:-1],
        padded[:, :, 2:, 1:-1, 1:-1],
        padded[:, :, 1:-1, :-2, 1:-1],
        padded[:, :, 1:-1, 2:, 1:-1],
        padded[:, :, 1:-1, 1:-1, :-2],
        padded[:, :, 1:-1, 1:-1, 2:],
    ]
    result = jnp.zeros(shifted[0].shape, jnp.float32)
    for direction in range(6):
        result = result + jnp.einsum(
            "vw,nwxyz->nvxyz",
            couplings[direction],
            shifted[direction],
            precision=lax.Precision.HIGHEST,
        )
    return result


def solve_blocks(blocks, right):
    size = blocks.shape[1]
    matrix = [[blocks[:, row, column] for column in range(size)] for row in range(size)]
    vector = [right[:, row] for row in range(size)]
    for pivot in range(size):
        for target in range(pivot + 1, size):
            factor = matrix[target][pivot] / matrix[pivot][pivot]
            for column in range(pivot + 1, size):
                matrix[target][column] = matrix[target][column] - factor * matrix[pivot][column]
            vector[target] = vector[target] - factor * vector[pivot]
    result = [None] * size
    for pivot in reversed(range(size)):
        total = vector[pivot]
        for column in range(pivot + 1, size):
            total = total - matrix[pivot][column] * result[column]
        result[pivot] = total / matrix[pivot][pivot]
    return jnp.stack(result, axis=1)


def spectral_term(field, local, ranks):
    total = local * ranks
    first = lax.axis_index("inst") * local
    own_rows = first + jnp.arange(local, dtype=jnp.int32)
    piece = lax.all_gather(field, "inst", axis=0, tiled=True)
    columns = jnp.arange(piece.shape[0], dtype=jnp.int32)
    return apply_table(spectral_table(own_rows, columns, total), piece)


def sweep(current, padded_xy, blocks, right_side, couplings, spectral):
    padded = jnp.pad(padded_xy, ((0, 0), (0, 0), (0, 0), (0, 0), (1, 1)))
    beside = neighbours(padded, couplings)
    diagonal_part = jnp.einsum(
        "nvwxyz,nwxyz->nvxyz", blocks, current, precision=lax.Precision.HIGHEST
    )
    resid = right_side - diagonal_part - beside - spectral
    return (current + solve_blocks(blocks, resid), resid)


def shards(state, source, jacobian, couplings, omega):
    ranks = lax.axis_size("inst")
    local, nvar, extent_x, extent_y, extent_z = state.shape
    current = state
    residual = state
    for repeat in range(ITERS):
        spectral = omega[0] * spectral_term(current, local, ranks)
        rows_ext = with_halo(current, (("gx", 2),), 1, False)
        both_ext = with_halo(rows_ext, (("gy", 3),), 1, True)
        current, residual = sweep(current, both_ext, jacobian, source, couplings, spectral)
    return (current, residual)


def solution(mesh):
    return jax.shard_map(
        shards,
        mesh=mesh,
        in_specs=(
            P("inst", None, "gx", "gy", None),
            P("inst", None, "gx", "gy", None),
            P("inst", None, None, "gx", "gy", None),
            P(),
            P(),
        ),
        out_specs=(P("inst", None, "gx", "gy", None), P("inst", None, "gx", "gy", None)),
        check_vma=False,
    )
```

profile of v0, /device:TPU:0, one launch (start us, length us, event | category | flops | bytes accessed | tf_op | source)
XLA Modules:
  0.0 110.3 jit_solution(15213774315029949874)
XLA Ops:
  9.2 4.9 %collective-permute-start = (f32[2,5,1,8,128]{4,1,3,2,0:T(8,128)S(1)}, f32[2,5,1,8,128]{4,1,3,2,0:T(8,128)S(1)}, u32[]{:S(2)}, u32[]{:S(2)}) collective-permute-start(f32[2,5,1,8,128]{4,1,3,2,0:T(8,128)S(1)} %get-tuple-element.56), channel_id=1, source_target_pairs={{0,4},{1,5},{2,6},{3,7},{8,12},{9,13},{10,14},{11,15},{16,20},{17,... | collective-permute-start | bytes 122888 | tf_op jit(solution)/shard_map/ppermute | solution.py:16
  14.1 1.3 %collective-permute-start.1 = (f32[2,5,1,8,128]{4,1,3,2,0:T(8,128)S(1)}, f32[2,5,1,8,128]{4,1,3,2,0:T(8,128)S(1)}, u32[]{:S(2)}, u32[]{:S(2)}) collective-permute-start(f32[2,5,1,8,128]{4,1,3,2,0:T(8,128)S(1)} %get-tuple-element.55), channel_id=1, source_target_pairs={{4,0},{5,1},{6,2},{7,3},{12,8},{13,9},{14,10},{15,11},{20,16},{21,... | collective-permute-start | bytes 122888 | tf_op jit(solution)/shard_map/ppermute | solution.py:19
  16.4 2.4 %multiply_reduce_fusion.2 = f32[2,8,8,128,5]{3,2,1,4,0:T(8,128)} fusion(f32[2,5,5,8,8,128]{5,4,3,2,1,0:T(8,128)} %param.7, f32[2,8,8,128,5]{3,2,1,4,0:T(8,128)S(1)} %bitcast.414), kind=kLoop, calls=%fused_computation.16 | loop fusion | flops 737280 | bytes 2293760 | tf_op jit(solution)/shard_map/nvwxyz,nwxyz->nvxyz/dot_general | solution.py:88
  20.2 3.7 %collective-permute-start.3 = (f32[2,5,10,1,128]{4,1,3,2,0:T(8,128)S(1)}, f32[2,5,10,1,128]{4,1,3,2,0:T(8,128)S(1)}, u32[]{:S(2)}, u32[]{:S(2)}) collective-permute-start(f32[2,5,10,1,128]{4,1,3,2,0:T(8,128)S(1)} %get-tuple-element.54), channel_id=1, source_target_pairs={{1,0},{2,1},{3,2},{0,3},{5,4},{6,5},{7,6},{4,7},{9,8},{10,9},{11,1... | collective-permute-start | bytes 153608 | tf_op jit(solution)/shard_map/ppermute | solution.py:19
  26.0 4.2 %collective-permute-done.2 = f32[2,5,10,1,128]{4,1,3,2,0:T(8,128)S(1)} collective-permute-done((f32[2,5,10,1,128]{4,1,3,2,0:T(8,128)S(1)}, f32[2,5,10,1,128]{4,1,3,2,0:T(8,128)S(1)}, u32[]{:S(2)}, u32[]{:S(2)}) %collective-permute-start.2) | collective-permute-done | bytes 51232 | tf_op jit(solution)/shard_map/ppermute | solution.py:16
  30.6 1.4 %fusion.12 = f32[2,8,8,128,5]{3,4,2,1,0:T(8,128)} fusion(f32[2,5,10,1,128]{4,1,3,2,0:T(8,128)S(1)} %collective-permute-done.3, f32[2,5,10,8,128]{4,1,3,2,0:T(8,128)S(1)} %constant_dynamic-update-slice_fusion, f32[1,5,5]{2,0,1:T(1,128)S(1)} %get-tuple-element.75), kind=kOutput, calls=%fused_computation.29 | convolution fusion | flops 5030400 | bytes 788580 | tf_op jit(solution)/shard_map/vw,nwxyz->nvxyz/dot_general | solution.py:48
  32.0 1.4 %fusion.8 = f32[2,8,8,128,5]{3,4,2,1,0:T(8,128)} fusion(f32[2,5,10,8,128]{4,1,3,2,0:T(8,128)S(1)} %constant_dynamic-update-slice_fusion, f32[2,5,10,1,128]{4,1,3,2,0:T(8,128)S(1)} %collective-permute-done.2, f32[1,5,5]{2,0,1:T(1,128)S(1)} %get-tuple-element.76), kind=kOutput, calls=%fused_computation.25 | convolution fusion | flops 5030400 | bytes 788580 | tf_op jit(solution)/shard_map/vw,nwxyz->nvxyz/dot_general | solution.py:48
  33.4 1.5 %fusion.24 = f32[2,8,8,128,5]{3,4,2,1,0:T(8,128)} fusion(f32[2,5,10,10,130]{4,1,3,2,0:T(8,128)S(1)} %select_maximum_fusion.8, f32[1,5,5]{2,0,1:T(1,128)S(1)} %get-tuple-element.78), kind=kOutput, calls=%fused_computation.41 | convolution fusion | flops 4915200 | bytes 854528 | tf_op jit(solution)/shard_map/vw,nwxyz->nvxyz/dot_general | solution.py:48
  34.9 1.4 %fusion.26 = f32[2,8,8,128,5]{3,4,2,1,0:T(8,128)} fusion(f32[2,5,10,10,130]{4,1,3,2,0:T(8,128)S(1)} %select_maximum_fusion.8, f32[1,5,5]{2,0,1:T(1,128)S(1)} %get-tuple-element.74), kind=kOutput, calls=%fused_computation.43 | convolution fusion | flops 4915200 | bytes 854528 | tf_op jit(solution)/shard_map/vw,nwxyz->nvxyz/dot_general | solution.py:48
  36.3 3.3 %fusion.6 = f32[2,5,8,8,128]{4,0,3,2,1:T(2,128)S(1)} fusion(f32[8,5,8,8,128]{4,3,2,1,0:T(8,128)} %all-gather.4.cloned.1.call-done, s32[2]{0:T(128)S(1)} %iota_add_fusion), kind=kOutput, calls=%fused_computation.23 | convolution fusion | flops 7864688 | bytes 1638408 | tf_op jit(solution)/shard_map/nm,mvxyz->nvxyz/dot_general | solution.py:34
  39.6 1.8 %fusion.54 = f32[2,5,8,8,128]{4,3,2,1,0:T(8,128)S(1)} fusion(f32[2,5,8,8,128]{4,3,2,1,0:T(8,128)S(1)} %copy-done.6, f32[2,8,8,128,5]{3,2,1,4,0:T(8,128)} %multiply_reduce_fusion.2, f32[2,5,8,8,128]{4,0,3,2,1:T(2,128)S(1)} %fusion.6, f32[2,8,8,128,5]{3,4,2,1,0:T(8,128)S(1)} %copy-done.13, f32[2,8,8,128,5]{3,4,2,1,0:T(8,128)S(1)} %copy-done.14, ...), kind=kLoop, calls=%fused_computation.92 | loop fusion | flops 737280 | bytes 3276804 | tf_op jit(solution)/shard_map/sub | solution.py:91
  44.1 4.5 %collective-permute-start.4 = (f32[2,5,1,8,128]{4,3,2,1,0:T(8,128)S(1)}, f32[2,5,1,8,128]{4,3,2,1,0:T(8,128)S(1)}, u32[]{:S(2)}, u32[]{:S(2)}) collective-permute-start(f32[2,5,1,8,128]{4,3,2,1,0:T(8,128)S(1)} %get-tuple-element.71), channel_id=1, source_target_pairs={{0,4},{1,5},{2,6},{3,7},{8,12},{9,13},{10,14},{11,15},{16,20},{17,... | collective-permute-start | bytes 122888 | tf_op jit(solution)/shard_map/ppermute | solution.py:16
  48.7 1.5 %collective-permute-done.4 = f32[2,5,1,8,128]{4,3,2,1,0:T(8,128)S(1)} collective-permute-done((f32[2,5,1,8,128]{4,3,2,1,0:T(8,128)S(1)}, f32[2,5,1,8,128]{4,3,2,1,0:T(8,128)S(1)}, u32[]{:S(2)}, u32[]{:S(2)}) %collective-permute-start.4) | collective-permute-done | bytes 40992 | tf_op jit(solution)/shard_map/ppermute | solution.py:16
  51.6 2.0 %collective-permute-start.6 = (f32[2,5,10,1,128]{4,3,2,1,0:T(1,128)S(1)}, f32[2,5,10,1,128]{4,3,2,1,0:T(1,128)S(1)}, u32[]{:S(2)}, u32[]{:S(2)}) collective-permute-start(f32[2,5,10,1,128]{4,3,2,1,0:T(1,128)S(1)} %get-tuple-element.63), channel_id=1, source_target_pairs={{0,1},{1,2},{2,3},{3,0},{4,5},{5,6},{6,7},{7,4},{8,9},{9,10},{10,1... | collective-permute-start | bytes 153608 | tf_op jit(solution)/shard_map/ppermute | solution.py:16
  53.6 1.9 %multiply_reduce_fusion.1 = f32[2,8,8,128,5]{3,2,1,4,0:T(8,128)} fusion(f32[2,5,5,8,8,128]{5,4,3,2,1,0:T(8,128)S(1)} %copy-done, f32[2,8,8,128,5]{3,2,1,4,0:T(8,128)} %bitcast.413), kind=kLoop, calls=%fused_computation.15 | loop fusion | flops 737280 | bytes 2293760 | tf_op jit(solution)/shard_map/nvwxyz,nwxyz->nvxyz/dot_general | solution.py:88
  55.7 2.0 %collective-permute-done.6 = f32[2,5,10,1,128]{4,3,2,1,0:T(1,128)S(1)} collective-permute-done((f32[2,5,10,1,128]{4,3,2,1,0:T(1,128)S(1)}, f32[2,5,10,1,128]{4,3,2,1,0:T(1,128)S(1)}, u32[]{:S(2)}, u32[]{:S(2)}) %collective-permute-start.6) | collective-permute-done | bytes 51232 | tf_op jit(solution)/shard_map/ppermute | solution.py:16
  60.5 1.6 %fusion.44 = f32[2,8,8,128,5]{3,4,2,1,0:T(8,128)} fusion(f32[2,5,8,8,128]{4,3,2,1,0:T(8,128)S(1)} %get-tuple-element.62, f32[1,5,5]{2,0,1:T(1,128)S(1)} %get-tuple-element.75), kind=kOutput, calls=%fused_computation.61 | convolution fusion | flops 4915200 | bytes 655460 | tf_op jit(solution)/shard_map/vw,nwxyz->nvxyz/dot_general | solution.py:48
  62.1 1.6 %fusion.46 = f32[2,8,8,128,5]{3,4,2,1,0:T(8,128)} fusion(f32[2,5,8,8,128]{4,3,2,1,0:T(8,128)S(1)} %get-tuple-element.61, f32[1,5,5]{2,0,1:T(1,128)S(1)} %get-tuple-element.76), kind=kOutput, calls=%fused_computation.63 | convolution fusion | flops 4915200 | bytes 655460 | tf_op jit(solution)/shard_map/vw,nwxyz->nvxyz/dot_general | solution.py:48
  63.6 1.6 %fusion.48 = f32[2,8,8,128,5]{3,4,2,1,0:T(8,128)} fusion(f32[2,5,8,8,128]{4,3,2,1,0:T(8,128)S(1)} %get-tuple-element.68, f32[1,5,5]{2,0,1:T(1,128)S(1)} %get-tuple-element.77), kind=kOutput, calls=%fused_computation.65 | convolution fusion | flops 4915200 | bytes 655460 | tf_op jit(solution)/shard_map/vw,nwxyz->nvxyz/dot_general | solution.py:48
  65.2 1.5 %fusion.50 = f32[2,8,8,128,5]{3,4,2,1,0:T(8,128)} fusion(f32[2,5,8,8,128]{4,3,2,1,0:T(8,128)S(1)} %get-tuple-element.67, f32[1,5,5]{2,0,1:T(1,128)S(1)} %get-tuple-element.73), kind=kOutput, calls=%fused_computation.67 | convolution fusion | flops 4915200 | bytes 655460 | tf_op jit(solution)/shard_map/vw,nwxyz->nvxyz/dot_general | solution.py:48
  66.7 3.3 %fusion.4 = f32[2,5,8,8,128]{4,0,3,2,1:T(2,128)S(1)} fusion(f32[8,5,8,8,128]{4,3,2,1,0:T(8,128)} %all-gather.6.cloned.1.call-done, s32[2]{0:T(128)} %copy-done.60), kind=kOutput, calls=%fused_computation.21 | convolution fusion | flops 7864688 | bytes 1638408 | tf_op jit(solution)/shard_map/nm,mvxyz->nvxyz/dot_general | solution.py:34
  70.3 1.7 %fusion.53 = f32[2,5,8,8,128]{4,3,2,1,0:T(8,128)S(1)} fusion(f32[2,5,8,8,128]{4,3,2,1,0:T(8,128)S(1)} %copy-done.6, f32[2,8,8,128,5]{3,2,1,4,0:T(8,128)} %multiply_reduce_fusion.1, f32[2,5,8,8,128]{4,0,3,2,1:T(2,128)S(1)} %fusion.4, f32[2,8,8,128,5]{3,4,2,1,0:T(8,128)S(1)} %fusion.40, f32[2,8,8,128,5]{3,4,2,1,0:T(8,128)S(1)} %fusion.42, ...), kind=kLoop, calls=%fused_computation.89 | loop fusion | flops 737280 | bytes 3276804 | tf_op jit(solution)/shard_map/sub | solution.py:91
  73.8 4.5 %collective-permute-start.8 = (f32[2,5,1,8,128]{4,3,2,1,0:T(8,128)S(1)}, f32[2,5,1,8,128]{4,3,2,1,0:T(8,128)S(1)}, u32[]{:S(2)}, u32[]{:S(2)}) collective-permute-start(f32[2,5,1,8,128]{4,3,2,1,0:T(8,128)S(1)} %get-tuple-element.69), channel_id=1, source_target_pairs={{0,4},{1,5},{2,6},{3,7},{8,12},{9,13},{10,14},{11,15},{16,20},{17,... | collective-permute-start | bytes 122888 | tf_op jit(solution)/shard_map/ppermute | solution.py:16
  78.4 1.6 %collective-permute-done.8 = f32[2,5,1,8,128]{4,3,2,1,0:T(8,128)S(1)} collective-permute-done((f32[2,5,1,8,128]{4,3,2,1,0:T(8,128)S(1)}, f32[2,5,1,8,128]{4,3,2,1,0:T(8,128)S(1)}, u32[]{:S(2)}, u32[]{:S(2)}) %collective-permute-start.8) | collective-permute-done | bytes 40992 | tf_op jit(solution)/shard_map/ppermute | solution.py:16
  83.3 1.9 %multiply_reduce_fusion = f32[2,8,8,128,5]{3,2,1,4,0:T(8,128)} fusion(f32[2,5,5,8,8,128]{5,4,3,2,1,0:T(8,128)S(1)} %copy-done, f32[2,8,8,128,5]{3,2,1,4,0:T(8,128)} %bitcast.412), kind=kLoop, calls=%fused_computation.14 | loop fusion | flops 737280 | bytes 2293760 | tf_op jit(solution)/shard_map/nvwxyz,nwxyz->nvxyz/dot_general | solution.py:88
  85.4 2.6 %collective-permute-done.10 = f32[2,5,10,1,128]{4,3,2,1,0:T(1,128)S(1)} collective-permute-done((f32[2,5,10,1,128]{4,3,2,1,0:T(1,128)S(1)}, f32[2,5,10,1,128]{4,3,2,1,0:T(1,128)S(1)}, u32[]{:S(2)}, u32[]{:S(2)}) %collective-permute-start.10) | collective-permute-done | bytes 51232 | tf_op jit(solution)/shard_map/ppermute | solution.py:16
  90.8 1.6 %fusion.32 = f32[2,8,8,128,5]{3,4,2,1,0:T(8,128)} fusion(f32[2,5,8,8,128]{4,3,2,1,0:T(8,128)S(1)} %get-tuple-element.58, f32[1,5,5]{2,0,1:T(1,128)S(1)} %get-tuple-element.75), kind=kOutput, calls=%fused_computation.49 | convolution fusion | flops 4915200 | bytes 655460 | tf_op jit(solution)/shard_map/vw,nwxyz->nvxyz/dot_general | solution.py:48
  92.4 1.6 %fusion.34 = f32[2,8,8,128,5]{3,4,2,1,0:T(8,128)} fusion(f32[2,5,8,8,128]{4,3,2,1,0:T(8,128)S(1)} %get-tuple-element.57, f32[1,5,5]{2,0,1:T(1,128)S(1)} %get-tuple-element.76), kind=kOutput, calls=%fused_computation.51 | convolution fusion | flops 4915200 | bytes 655460 | tf_op jit(solution)/shard_map/vw,nwxyz->nvxyz/dot_general | solution.py:48
  93.9 1.6 %fusion.36 = f32[2,8,8,128,5]{3,4,2,1,0:T(8,128)} fusion(f32[2,5,8,8,128]{4,3,2,1,0:T(8,128)S(1)} %get-tuple-element.66, f32[1,5,5]{2,0,1:T(1,128)S(1)} %get-tuple-element.77), kind=kOutput, calls=%fused_computation.53 | convolution fusion | flops 4915200 | bytes 655460 | tf_op jit(solution)/shard_map/vw,nwxyz->nvxyz/dot_general | solution.py:48
  95.5 1.6 %fusion.38 = f32[2,8,8,128,5]{3,4,2,1,0:T(8,128)} fusion(f32[2,5,8,8,128]{4,3,2,1,0:T(8,128)S(1)} %get-tuple-element.65, f32[1,5,5]{2,0,1:T(1,128)S(1)} %get-tuple-element.73), kind=kOutput, calls=%fused_computation.55 | convolution fusion | flops 4915200 | bytes 655460 | tf_op jit(solution)/shard_map/vw,nwxyz->nvxyz/dot_general | solution.py:48
  97.0 3.3 %fusion.2 = f32[2,5,8,8,128]{4,0,3,2,1:T(2,128)S(1)} fusion(f32[8,5,8,8,128]{4,3,2,1,0:T(8,128)} %all-gather.8.cloned.1.call-done, s32[2]{0:T(128)S(1)} %copy-done.61), kind=kOutput, calls=%fused_computation.19 | convolution fusion | flops 7864688 | bytes 1638408 | tf_op jit(solution)/shard_map/nm,mvxyz->nvxyz/dot_general | solution.py:34
  100.6 1.7 %fusion.52 = f32[2,5,8,8,128]{4,3,2,1,0:T(8,128)S(1)} fusion(f32[2,5,8,8,128]{4,3,2,1,0:T(8,128)S(1)} %copy-done.6, f32[2,8,8,128,5]{3,2,1,4,0:T(8,128)} %multiply_reduce_fusion, f32[2,5,8,8,128]{4,0,3,2,1:T(2,128)S(1)} %fusion.2, f32[2,8,8,128,5]{3,4,2,1,0:T(8,128)S(1)} %fusion.28, f32[2,8,8,128,5]{3,4,2,1,0:T(8,128)S(1)} %fusion.30, ...), kind=kLoop, calls=%fused_computation.86 | loop fusion | flops 737280 | bytes 3276804 | tf_op jit(solution)/shard_map/sub | solution.py:91
  (192 shorter events, 22.3 us)
Async XLA Ops:
  7.2 9.2 %copy-start.5 = (f32[2,5,8,8,128]{4,3,2,1,0:T(8,128)S(1)}, f32[2,5,8,8,128]{4,3,2,1,0:T(8,128)}, u32[]{:S(2)}) copy-start(f32[2,5,8,8,128]{4,3,2,1,0:T(8,128)} %param.5) | copy-start | bytes 983044
  7.2 29.1 %all-gather.4.cloned.1.call-start = ((), (), s32[]{:S(2)}) async-start(), calls=%async_computation | async-start | bytes 1638400 | tf_op jit(solution)/shard_map/all_gather | solution.py:80
  7.9 58.8 %all-gather.6.cloned.1.call-start = ((), (), s32[]{:S(2)}) async-start(), calls=%async_computation.1 | async-start | bytes 1638400 | tf_op jit(solution)/shard_map/all_gather | solution.py:80
  9.2 10.3 %collective-permute-start = (f32[2,5,1,8,128]{4,1,3,2,0:T(8,128)S(1)}, f32[2,5,1,8,128]{4,1,3,2,0:T(8,128)S(1)}, u32[]{:S(2)}, u32[]{:S(2)}) collective-permute-start(f32[2,5,1,8,128]{4,1,3,2,0:T(8,128)S(1)} %get-tuple-element.56), channel_id=1, source_target_pairs={{0,4},{1,5},{2,6},{3,7},{8,12},{9,13},{10,14},{11,15},{16,20},{17,... | collective-permute-start | bytes 122888 | tf_op jit(solution)/shard_map/ppermute | solution.py:16
  14.1 6.2 %collective-permute-start.1 = (f32[2,5,1,8,128]{4,1,3,2,0:T(8,128)S(1)}, f32[2,5,1,8,128]{4,1,3,2,0:T(8,128)S(1)}, u32[]{:S(2)}, u32[]{:S(2)}) collective-permute-start(f32[2,5,1,8,128]{4,1,3,2,0:T(8,128)S(1)} %get-tuple-element.55), channel_id=1, source_target_pairs={{4,0},{5,1},{6,2},{7,3},{12,8},{13,9},{14,10},{15,11},{20,16},{21,... | collective-permute-start | bytes 122888 | tf_op jit(solution)/shard_map/ppermute | solution.py:19
  16.3 17.1 %copy-start.57 = (f32[1,5,5]{2,0,1:T(1,128)}, f32[1,5,5]{2,0,1:T(1,128)S(1)}, u32[]{:S(2)}) copy-start(f32[1,5,5]{2,0,1:T(1,128)S(1)} %get-tuple-element.78) | copy-start | bytes 304
  16.4 18.6 %copy-start.54 = (f32[1,5,5]{2,0,1:T(1,128)}, f32[1,5,5]{2,0,1:T(1,128)S(1)}, u32[]{:S(2)}) copy-start(f32[1,5,5]{2,0,1:T(1,128)S(1)} %get-tuple-element.74) | copy-start | bytes 304
  18.8 17.5 %copy-start.60 = (s32[2]{0:T(128)}, s32[2]{0:T(128)S(1)}, u32[]{:S(2)}) copy-start(s32[2]{0:T(128)S(1)} %iota_add_fusion) | copy-start | bytes 28
  20.2 5.7 %collective-permute-start.3 = (f32[2,5,10,1,128]{4,1,3,2,0:T(8,128)S(1)}, f32[2,5,10,1,128]{4,1,3,2,0:T(8,128)S(1)}, u32[]{:S(2)}, u32[]{:S(2)}) collective-permute-start(f32[2,5,10,1,128]{4,1,3,2,0:T(8,128)S(1)} %get-tuple-element.54), channel_id=1, source_target_pairs={{1,0},{2,1},{3,2},{0,3},{5,4},{6,5},{7,6},{4,7},{9,8},{10,9},{11,1... | collective-permute-start | bytes 153608 | tf_op jit(solution)/shard_map/ppermute | solution.py:19
  23.9 6.2 %collective-permute-start.2 = (f32[2,5,10,1,128]{4,1,3,2,0:T(8,128)S(1)}, f32[2,5,10,1,128]{4,1,3,2,0:T(8,128)S(1)}, u32[]{:S(2)}, u32[]{:S(2)}) collective-permute-start(f32[2,5,10,1,128]{4,1,3,2,0:T(8,128)S(1)} %get-tuple-element.53), channel_id=1, source_target_pairs={{0,1},{1,2},{2,3},{3,0},{4,5},{5,6},{6,7},{7,4},{8,9},{9,10},{10,1... | collective-permute-start | bytes 153608 | tf_op jit(solution)/shard_map/ppermute | solution.py:16
  33.4 6.2 %copy-start.6 = (f32[2,5,8,8,128]{4,3,2,1,0:T(8,128)S(1)}, f32[2,5,8,8,128]{4,3,2,1,0:T(8,128)}, u32[]{:S(2)}) copy-start(f32[2,5,8,8,128]{4,3,2,1,0:T(8,128)} %param.6) | copy-start | bytes 983044
  36.3 3.3 %copy-start.14 = (f32[2,8,8,128,5]{3,4,2,1,0:T(8,128)S(1)}, f32[2,8,8,128,5]{3,4,2,1,0:T(8,128)}, u32[]{:S(2)}) copy-start(f32[2,8,8,128,5]{3,4,2,1,0:T(8,128)} %fusion.26) | copy-start | bytes 983044
  42.8 5.9 %copy-start.3 = (f32[2,5,8,8,128]{4,3,2,1,0:T(8,128)}, f32[2,5,8,8,128]{4,3,2,1,0:T(8,128)S(1)}, u32[]{:S(2)}) copy-start(f32[2,5,8,8,128]{4,3,2,1,0:T(8,128)S(1)} %add.111) | copy-start | bytes 983044
  42.8 6.0 %collective-permute-start.5 = (f32[2,5,1,8,128]{4,3,2,1,0:T(8,128)S(1)}, f32[2,5,1,8,128]{4,3,2,1,0:T(8,128)S(1)}, u32[]{:S(2)}, u32[]{:S(2)}) collective-permute-start(f32[2,5,1,8,128]{4,3,2,1,0:T(8,128)S(1)} %get-tuple-element.72), channel_id=1, source_target_pairs={{4,0},{5,1},{6,2},{7,3},{12,8},{13,9},{14,10},{15,11},{20,16},{21,... | collective-permute-start | bytes 122888 | tf_op jit(solution)/shard_map/ppermute | solution.py:19
  44.1 6.2 %collective-permute-start.4 = (f32[2,5,1,8,128]{4,3,2,1,0:T(8,128)S(1)}, f32[2,5,1,8,128]{4,3,2,1,0:T(8,128)S(1)}, u32[]{:S(2)}, u32[]{:S(2)}) collective-permute-start(f32[2,5,1,8,128]{4,3,2,1,0:T(8,128)S(1)} %get-tuple-element.71), channel_id=1, source_target_pairs={{0,4},{1,5},{2,6},{3,7},{8,12},{9,13},{10,14},{11,15},{16,20},{17,... | collective-permute-start | bytes 122888 | tf_op jit(solution)/shard_map/ppermute | solution.py:16
  48.7 9.0 %copy-start.4 = (f32[2,5,8,8,128]{4,3,2,1,0:T(8,128)S(1)}, f32[2,5,8,8,128]{4,3,2,1,0:T(8,128)}, u32[]{:S(2)}) copy-start(f32[2,5,8,8,128]{4,3,2,1,0:T(8,128)} %copy-done.3) | copy-start | bytes 983044
  48.7 48.3 %all-gather.8.cloned.1.call-start = ((), (), s32[]{:S(2)}) async-start(), calls=%async_computation.2 | async-start | bytes 1638400 | tf_op jit(solution)/shard_map/all_gather | solution.py:80
  51.5 4.2 %collective-permute-start.7 = (f32[2,5,10,1,128]{4,3,2,1,0:T(1,128)S(1)}, f32[2,5,10,1,128]{4,3,2,1,0:T(1,128)S(1)}, u32[]{:S(2)}, u32[]{:S(2)}) collective-permute-start(f32[2,5,10,1,128]{4,3,2,1,0:T(1,128)S(1)} %get-tuple-element.64), channel_id=1, source_target_pairs={{1,0},{2,1},{3,2},{0,3},{5,4},{6,5},{7,6},{4,7},{9,8},{10,9},{11,1... | collective-permute-start | bytes 153608 | tf_op jit(solution)/shard_map/ppermute | solution.py:19
  51.6 6.1 %collective-permute-start.6 = (f32[2,5,10,1,128]{4,3,2,1,0:T(1,128)S(1)}, f32[2,5,10,1,128]{4,3,2,1,0:T(1,128)S(1)}, u32[]{:S(2)}, u32[]{:S(2)}) collective-permute-start(f32[2,5,10,1,128]{4,3,2,1,0:T(1,128)S(1)} %get-tuple-element.63), channel_id=1, source_target_pairs={{0,1},{1,2},{2,3},{3,0},{4,5},{5,6},{6,7},{7,4},{8,9},{9,10},{10,1... | collective-permute-start | bytes 153608 | tf_op jit(solution)/shard_map/ppermute | solution.py:16
  66.7 3.4 %copy-start.10 = (f32[2,8,8,128,5]{3,4,2,1,0:T(8,128)S(1)}, f32[2,8,8,128,5]{3,4,2,1,0:T(8,128)}, u32[]{:S(2)}) copy-start(f32[2,8,8,128,5]{3,4,2,1,0:T(8,128)} %fusion.44) | copy-start | bytes 983044
  66.7 3.4 %copy-start.11 = (f32[2,8,8,128,5]{3,4,2,1,0:T(8,128)S(1)}, f32[2,8,8,128,5]{3,4,2,1,0:T(8,128)}, u32[]{:S(2)}) copy-start(f32[2,8,8,128,5]{3,4,2,1,0:T(8,128)} %fusion.46) | copy-start | bytes 983044
  66.7 3.4 %copy-start.12 = (f32[2,8,8,128,5]{3,4,2,1,0:T(8,128)S(1)}, f32[2,8,8,128,5]{3,4,2,1,0:T(8,128)}, u32[]{:S(2)}) copy-start(f32[2,8,8,128,5]{3,4,2,1,0:T(8,128)} %fusion.48) | copy-start | bytes 983044
  72.4 5.9 %copy-start.1 = (f32[2,5,8,8,128]{4,3,2,1,0:T(8,128)}, f32[2,5,8,8,128]{4,3,2,1,0:T(8,128)S(1)}, u32[]{:S(2)}) copy-start(f32[2,5,8,8,128]{4,3,2,1,0:T(8,128)S(1)} %add.118) | copy-start | bytes 983044
  72.5 5.9 %collective-permute-start.9 = (f32[2,5,1,8,128]{4,3,2,1,0:T(8,128)S(1)}, f32[2,5,1,8,128]{4,3,2,1,0:T(8,128)S(1)}, u32[]{:S(2)}, u32[]{:S(2)}) collective-permute-start(f32[2,5,1,8,128]{4,3,2,1,0:T(8,128)S(1)} %get-tuple-element.70), channel_id=1, source_target_pairs={{4,0},{5,1},{6,2},{7,3},{12,8},{13,9},{14,10},{15,11},{20,16},{21,... | collective-permute-start | bytes 122888 | tf_op jit(solution)/shard_map/ppermute | solution.py:19
  73.8 6.2 %collective-permute-start.8 = (f32[2,5,1,8,128]{4,3,2,1,0:T(8,128)S(1)}, f32[2,5,1,8,128]{4,3,2,1,0:T(8,128)S(1)}, u32[]{:S(2)}, u32[]{:S(2)}) collective-permute-start(f32[2,5,1,8,128]{4,3,2,1,0:T(8,128)S(1)} %get-tuple-element.69), channel_id=1, source_target_pairs={{0,4},{1,5},{2,6},{3,7},{8,12},{9,13},{10,14},{11,15},{16,20},{17,... | collective-permute-start | bytes 122888 | tf_op jit(solution)/shard_map/ppermute | solution.py:16
  78.4 9.6 %copy-start.2 = (f32[2,5,8,8,128]{4,3,2,1,0:T(8,128)S(1)}, f32[2,5,8,8,128]{4,3,2,1,0:T(8,128)}, u32[]{:S(2)}) copy-start(f32[2,5,8,8,128]{4,3,2,1,0:T(8,128)} %copy-done.1) | copy-start | bytes 983044
  81.2 4.2 %collective-permute-start.11 = (f32[2,5,10,1,128]{4,3,2,1,0:T(1,128)S(1)}, f32[2,5,10,1,128]{4,3,2,1,0:T(1,128)S(1)}, u32[]{:S(2)}, u32[]{:S(2)}) collective-permute-start(f32[2,5,10,1,128]{4,3,2,1,0:T(1,128)S(1)} %get-tuple-element.60), channel_id=1, source_target_pairs={{1,0},{2,1},{3,2},{0,3},{5,4},{6,5},{7,6},{4,7},{9,8},{10,9},{11,1... | collective-permute-start | bytes 153608 | tf_op jit(solution)/shard_map/ppermute | solution.py:19
  82.1 5.9 %collective-permute-start.10 = (f32[2,5,10,1,128]{4,3,2,1,0:T(1,128)S(1)}, f32[2,5,10,1,128]{4,3,2,1,0:T(1,128)S(1)}, u32[]{:S(2)}, u32[]{:S(2)}) collective-permute-start(f32[2,5,10,1,128]{4,3,2,1,0:T(1,128)S(1)} %get-tuple-element.59), channel_id=1, source_target_pairs={{0,1},{1,2},{2,3},{3,0},{4,5},{5,6},{6,7},{7,4},{8,9},{9,10},{10,1... | collective-permute-start | bytes 153608 | tf_op jit(solution)/shard_map/ppermute | solution.py:16
  92.4 4.7 %copy-start.61 = (s32[2]{0:T(128)S(1)}, s32[2]{0:T(128)}, u32[]{:S(2)}) copy-start(s32[2]{0:T(128)} %copy-done.60) | copy-start | bytes 28
  97.0 3.4 %copy-start.7 = (f32[2,8,8,128,5]{3,4,2,1,0:T(8,128)S(1)}, f32[2,8,8,128,5]{3,4,2,1,0:T(8,128)}, u32[]{:S(2)}) copy-start(f32[2,8,8,128,5]{3,4,2,1,0:T(8,128)} %fusion.32) | copy-start | bytes 983044
  97.0 3.4 %copy-start.8 = (f32[2,8,8,128,5]{3,4,2,1,0:T(8,128)S(1)}, f32[2,8,8,128,5]{3,4,2,1,0:T(8,128)}, u32[]{:S(2)}) copy-start(f32[2,8,8,128,5]{3,4,2,1,0:T(8,128)} %fusion.34) | copy-start | bytes 983044
  97.0 3.4 %copy-start.9 = (f32[2,8,8,128,5]{3,4,2,1,0:T(8,128)S(1)}, f32[2,8,8,128,5]{3,4,2,1,0:T(8,128)}, u32[]{:S(2)}) copy-start(f32[2,8,8,128,5]{3,4,2,1,0:T(8,128)} %fusion.36) | copy-start | bytes 983044
  (45 other events, 76.9 us)
Sparse Core Ops, SparseCore 0:
  9.5 20.8 all-gather.3
  48.8 15.4 all-gather.5
  78.5 15.4 all-gather.7
where the time goes:
time: 111 us; the launch traced here: 110 us
  matrix products  32.2 us (29%)
  starting transfers between devices  25.8 us (23%)
  other arithmetic  18.7 us (17%)
  between operations  15.6 us (14%)
  waiting for transfers between devices  14.5 us (13%)
  local copies, waits for them, and re-layouts  3.4 us (3%)
    dot_general x18, matrix products, neighbours(): jnp.einsum('vw,nwxyz->nvxyz', couplings[direction], shifted[direction], p...  22.2 us
    ppermute x6, starting transfers between devices, with_halo(): lax.ppermute(lax.slice_in_dim(block, block.shape[dim] - width, None, axis...  17.2 us
    ppermute x6, waiting for transfers between devices, with_halo(): lax.ppermute(lax.slice_in_dim(block, block.shape[dim] - width, None, axis...  12 us
    dot_general x3, matrix products, apply_table(): jnp.einsum('nm,mvxyz->nvxyz', table, field, precision=lax.Precision.HIGHEST)  9.96 us
    ppermute x6, starting transfers between devices, with_halo(): lax.ppermute(lax.slice_in_dim(block, 0, width, axis=dim), axis, backward)  8.48 us
    dot_general x3, other arithmetic, sweep(): jnp.einsum('nvwxyz,nwxyz->nvxyz', blocks, current, precision=lax.Precisio...  6.23 us
    sub x3, other arithmetic, sweep(): resid = right_side - diagonal_part - beside - spectral  5.16 us
    concatenate x5, other arithmetic, with_halo(): block = jnp.concatenate([low, block, high], axis=dim)  2.6 us
  transfers between devices with their start and end apart: 15, of which 9 were waited for; matrix products, arithmetic and copies ran while one was open for 33% of the time, Pallas kernels for 0%

commit v1 on v0

v1 whole, which is shorter than its diff:
```python
import functools
import math

import jax
import jax.numpy as jnp
from jax import lax
from jax.experimental import pallas as pl
from jax.experimental.pallas import tpu as pltpu
from jax.sharding import PartitionSpec as P

ITERS = 3
MESH = pl.DeviceIdType.MESH


def derivative(offset, total):
    offset = offset % total
    if offset > total // 2:
        offset -= total
    if offset == 0:
        return 0.0
    angle = math.pi * offset / total
    return 0.5 * (-1.0) ** offset * math.cos(angle) / math.sin(angle)


def factor(blocks):
    size = len(blocks)
    matrix = [list(row) for row in blocks]
    for pivot in range(size):
        matrix[pivot][pivot] = 1.0 / matrix[pivot][pivot]
        for target in range(pivot + 1, size):
            ratio = matrix[target][pivot] * matrix[pivot][pivot]
            matrix[target][pivot] = ratio
            for column in range(pivot + 1, size):
                matrix[target][column] = matrix[target][column] - ratio * matrix[pivot][column]
    return matrix


def substitute(matrix, right):
    size = len(right)
    vector = list(right)
    for pivot in range(size):
        for target in range(pivot + 1, size):
            vector[target] = vector[target] - matrix(target, pivot) * vector[pivot]
    result = [None] * size
    for pivot in reversed(range(size)):
        total = vector[pivot]
        for column in range(pivot + 1, size):
            total = total - matrix(pivot, column) * result[column]
        result[pivot] = total * matrix(pivot, pivot)
    return result


def weighted(weights, pieces):
    total = None
    for weight, piece in zip(weights, pieces):
        if isinstance(weight, float) and weight == 0.0:
            continue
        term = weight * piece
        total = term if total is None else total + term
    return total


def kernel(
    ranks, count_x, count_y,
    state, source, jacobian, couplings, omega,
    state_next, last_residual,
    cur, peer, part, got, low_out, high_out, low_in, high_in,
    rhs, blocks, lu, final, resid,
    load_sem, peer_send, peer_recv, part_send, part_recv,
    edge_send, edge_recv, side_send, side_recv, store_sem,
):
    local, nvar, planes, rows, depth = state.shape
    total = local * ranks
    pairs = ranks // 2
    rank = lax.axis_index("inst")
    at_x = lax.axis_index("gx")
    at_y = lax.axis_index("gy")
    pair = rank // 2
    core = rank % 2
    partner = pair * 2 + 1 - core
    up = (at_y + 1) % count_y
    down = (at_y + count_y - 1) % count_y
    has_low = at_x > 0
    has_high = at_x < count_x - 1
    flip = at_x % 2 == 0

    def plane_of(step):
        return jnp.where(flip, planes - 1 - step, step)

    def load_state(x):
        return pltpu.make_async_copy(state.at[:, :, x], cur.at[0, x + 1], load_sem.at[0, x])

    def load_source(x):
        return pltpu.make_async_copy(source.at[:, :, x], rhs.at[x], load_sem.at[1, x])

    def load_blocks(x):
        return pltpu.make_async_copy(jacobian.at[:, :, :, x], blocks.at[x], load_sem.at[2, x])

    def store_state(x):
        return pltpu.make_async_copy(final.at[x], state_next.at[:, :, x], store_sem.at[0, x])

    def store_resid(x):
        return pltpu.make_async_copy(resid.at[x], last_residual.at[:, :, x], store_sem.at[1, x])

    def to_peer(k, x):
        return pltpu.make_async_remote_copy(
            cur.at[k, x + 1], peer.at[k, x], peer_send.at[k, x], peer_recv.at[k, x],
            device_id={"inst": partner}, device_id_type=MESH)

    def to_pair(k, x, hop):
        target = ((pair + hop) % pairs) * 2 + core
        return pltpu.make_async_remote_copy(
            part.at[k, hop - 1, x], got.at[k, hop - 1, x],
            part_send.at[k, hop - 1, x], part_recv.at[k, hop - 1, x],
            device_id={"inst": target}, device_id_type=MESH)

    def to_up(k, x):
        return pltpu.make_async_remote_copy(
            high_out.at[k, x], low_in.at[k, x], edge_send.at[0, k, x], edge_recv.at[0, k, x],
            device_id={"gy": up}, device_id_type=MESH)

    def to_down(k, x):
        return pltpu.make_async_remote_copy(
            low_out.at[k, x], high_in.at[k, x], edge_send.at[1, k, x], edge_recv.at[1, k, x],
            device_id={"gy": down}, device_id_type=MESH)

    def to_next(k):
        return pltpu.make_async_remote_copy(
            cur.at[k, planes], cur.at[k, 0], side_send.at[0, k], side_recv.at[0, k],
            device_id={"gx": at_x + 1}, device_id_type=MESH)

    def to_last(k):
        return pltpu.make_async_remote_copy(
            cur.at[k, 1], cur.at[k, planes + 1], side_send.at[1, k], side_recv.at[1, k],
            device_id={"gx": at_x - 1}, device_id_type=MESH)

    def send_planes(k, x):
        to_peer(k, x).start()

        @pl.when(jnp.logical_and(x == planes - 1, has_high))
        def _():
            to_next(k).start()

        @pl.when(jnp.logical_and(x == 0, has_low))
        def _():
            to_last(k).start()

    def send_edges(k, x, field):
        for n in range(local):
            for v in range(nvar):
                at = n * nvar + v
                low_out[k, x, at:at + 1] = field[n][v][:1]
                high_out[k, x, at:at + 1] = field[n][v][rows - 1:]

    def start_edges(k, x):
        to_up(k, x).start()
        to_down(k, x).start()

    def mine(k, x):
        return [[cur[k, x + 1, n, v] for v in range(nvar)] for n in range(local)]

    even = core == 0

    def weights_of(hop, a):
        own = [derivative(2 * local * hop + a - b, total) for b in range(local)]
        other = [
            jnp.where(
                even,
                jnp.float32(derivative(2 * local * hop - local + a - b, total)),
                jnp.float32(derivative(2 * local * hop + local + a - b, total)),
            )
            for b in range(local)
        ]
        return own + other

    def send_parts(k, x):
        to_peer(k, x).wait_recv()
        for hop in range(1, pairs):
            for a in range(local):
                weights = weights_of(hop, a)
                for v in range(nvar):
                    pieces = [cur[k, x + 1, b, v] for b in range(local)]
                    pieces += [peer[k, x, b, v] for b in range(local)]
                    part[k, hop - 1, x, a, v] = weighted(weights, pieces)
            to_pair(k, x, hop).start()

    for step in range(planes):
        load_state(plane_of(step)).start()
    for step in range(planes):
        load_blocks(plane_of(step)).start()
        load_source(plane_of(step)).start()

    barrier = pltpu.get_barrier_semaphore()

    def greet(**where):
        pl.semaphore_signal(barrier, inc=1, device_id=where, device_id_type=MESH)

    greet(inst=partner)
    for hop in range(1, pairs):
        greet(inst=((pair + hop) % pairs) * 2 + core)
    greet(gy=up)
    greet(gy=down)

    @pl.when(has_low)
    def _():
        greet(gx=at_x - 1)

    @pl.when(has_high)
    def _():
        greet(gx=at_x + 1)

    zero = jnp.zeros((local, nvar, rows, depth), jnp.float32)

    @pl.when(jnp.logical_not(has_low))
    def _():
        for k in range(ITERS):
            cur[k, 0] = zero

    @pl.when(jnp.logical_not(has_high))
    def _():
        for k in range(ITERS):
            cur[k, planes + 1] = zero

    sides = has_low.astype(jnp.int32) + has_high.astype(jnp.int32)
    pl.semaphore_wait(barrier, pairs + 2 + sides)

    @pl.loop(0, planes)
    def _(step):
        x = plane_of(step)
        load_state(x).wait()
        send_planes(0, x)

    @pl.loop(0, planes)
    def _(step):
        send_parts(0, plane_of(step))

    @pl.loop(0, planes)
    def _(step):
        x = plane_of(step)
        send_edges(0, x, mine(0, x))
        start_edges(0, x)

    row_at = lax.broadcasted_iota(jnp.int32, (rows, depth), 0)
    lane_at = lax.broadcasted_iota(jnp.int32, (rows, depth), 1)
    first_row, final_row = row_at == 0, row_at == rows - 1
    first_lane, final_lane = lane_at == 0, lane_at == depth - 1
    speed = omega[0]

    def right_side(k, x, n):
        result = []
        for v in range(nvar):
            result.append(None)
        for w in range(nvar):
            field = cur[k, x + 1, n, w]
            at = n * nvar + w
            shifted = [
                cur[k, x, n, w],
                cur[k, x + 2, n, w],
                jnp.where(first_row, low_in[k, x, at:at + 1], pltpu.roll(field, 1, 0)),
                jnp.where(final_row, high_in[k, x, at:at + 1], pltpu.roll(field, rows - 1, 0)),
                jnp.where(first_lane, 0.0, pltpu.roll(field, 1, 1)),
                jnp.where(final_lane, 0.0, pltpu.roll(field, depth - 1, 1)),
            ]
            for v in range(nvar):
                term = weighted([couplings[v, d, w] for d in range(6)], shifted)
                result[v] = term if result[v] is None else result[v] + term
        weights = weights_of(0, n)
        for v in range(nvar):
            pieces = [cur[k, x + 1, b, v] for b in range(local)]
            pieces += [peer[k, x, b, v] for b in range(local)]
            spectral = weighted(weights, pieces)
            for hop in range(1, pairs):
                spectral = spectral + got[k, hop - 1, x, n, v]
            result[v] = rhs[x, n, v] - result[v] - speed * spectral
        return result

    for k in range(ITERS):
        final_pass = k == ITERS - 1

        @pl.loop(0, planes)
        def _(step, k=k, final_pass=final_pass):
            x = plane_of(step)
            if k == 0:
                load_blocks(x).wait()
                for n in range(local):
                    matrix = factor(
                        [[blocks[x, n, v, w] for w in range(nvar)] for v in range(nvar)])
                    for v in range(nvar):
                        for w in range(nvar):
                            lu[x, n, v, w] = matrix[v][w]
                load_source(x).wait()

            @pl.when(jnp.logical_and(x == 0, has_low))
            def _():
                to_next(k).wait_recv()

            @pl.when(jnp.logical_and(x == planes - 1, has_high))
            def _():
                to_last(k).wait_recv()

            to_up(k, x).wait_recv()
            to_down(k, x).wait_recv()
            for hop in range(1, pairs):
                to_pair(k, x, hop).wait_recv()
            fields = []
            for n in range(local):
                right = right_side(k, x, n)
                if final_pass:
                    own = [cur[k, x + 1, n, w] for w in range(nvar)]
                    for v in range(nvar):
                        for w in range(nvar):
                            right[v] = right[v] - blocks[x, n, v, w] * own[w]
                        resid[x, n, v] = right[v]
                answer = substitute(lambda v, w: lu[x, n, v, w], right)
                if final_pass:
                    for v in range(nvar):
                        final[x, n, v] = own[v] + answer[v]
                else:
                    for v in range(nvar):
                        cur[k + 1, x + 1, n, v] = answer[v]
                    fields.append(answer)
            if final_pass:
                store_resid(x).start()
                store_state(x).start()
            else:
                send_edges(k + 1, x, fields)
                send_planes(k + 1, x)
                start_edges(k + 1, x)

                @pl.when(step > 0)
                def _():
                    send_parts(k + 1, plane_of(step - 1))

            if k > 0:

                @pl.when(step == 0)
                def _():
                    send_parts(k, plane_of(planes - 1))

    @pl.loop(0, planes)
    def _(x):
        for k in range(ITERS):
            to_peer(k, x).wait_send()
            for hop in range(1, pairs):
                to_pair(k, x, hop).wait_send()
            to_up(k, x).wait_send()
            to_down(k, x).wait_send()
        store_resid(x).wait()
        store_state(x).wait()

    for k in range(ITERS):

        @pl.when(has_high)
        def _():
            to_next(k).wait_send()

        @pl.when(has_low)
        def _():
            to_last(k).wait_send()


def solution(mesh):
    ranks, count_x, count_y = mesh.shape["inst"], mesh.shape["gx"], mesh.shape["gy"]

    def shards(state, source, jacobian, couplings, omega):
        local, nvar, planes, rows, depth = state.shape
        pairs = ranks // 2
        cell = (local, nvar, rows, depth)
        edge = pltpu.VMEM((ITERS, planes, local * nvar, depth), jnp.float32)
        hbm = pl.BlockSpec(memory_space=pl.ANY)
        smem = pl.BlockSpec(memory_space=pltpu.SMEM)
        dma = pltpu.SemaphoreType.DMA
        vmem = lambda *lead: pltpu.VMEM(lead + cell, jnp.float32)
        matrices = pltpu.VMEM((planes, local, nvar, nvar, rows, depth), jnp.float32)
        return tuple(pl.pallas_call(
            functools.partial(kernel, ranks, count_x, count_y),
            out_shape=[jax.ShapeDtypeStruct(state.shape, jnp.float32)] * 2,
            in_specs=[hbm, hbm, hbm, smem, smem],
            out_specs=[hbm, hbm],
            scratch_shapes=[
                vmem(ITERS, planes + 2), vmem(ITERS, planes),
                vmem(ITERS, pairs - 1, planes), vmem(ITERS, pairs - 1, planes),
                edge, edge, edge, edge,
                vmem(planes), matrices, matrices, vmem(planes), vmem(planes),
                dma((3, planes)), dma((ITERS, planes)), dma((ITERS, planes)),
                dma((ITERS, pairs - 1, planes)), dma((ITERS, pairs - 1, planes)),
                dma((2, ITERS, planes)), dma((2, ITERS, planes)),
                dma((2, ITERS)), dma((2, ITERS)), dma((2, planes)),
            ],
            compiler_params=pltpu.CompilerParams(
                collective_id=0, has_side_effects=True, vmem_limit_bytes=48 * 2**20),
            name="smooth",
        )(state, source, jacobian, couplings.transpose(1, 0, 2), omega))

    split = P("inst", None, "gx", "gy", None)
    return jax.shard_map(
        shards,
        mesh=mesh,
        in_specs=(split, split, P("inst", None, None, "gx", "gy", None), P(), P()),
        out_specs=(split, split),
        check_vma=False,
    )
```

time: 111 us -> 40.2 us (0.36)
  Pallas kernels: 0 us -> 33.1 us
  matrix products: 32.2 us -> 0 us
  starting transfers between devices: 25.8 us -> 0 us
  other arithmetic: 18.7 us -> 0 us
  waiting for transfers between devices: 14.5 us -> 0 us
  between operations: 15.6 us -> 1.3 us
  local copies, waits for them, and re-layouts: 3.4 us -> 5.55 us
    pallas_call x0 -> x1, Pallas kernels: none -> 33.1 us  [shards(): pl.pallas_call(functools.partial(kernel, ranks, count_x, count_y), out_sh...]
    dot_general x21 -> x0, matrix products: 32.2 us -> none  [the longest x18 22.2 us: neighbours(): jnp.einsum('vw,nwxyz->nvxyz', couplings[direction], shifted[direction], p...]
    ppermute x12 -> x0, starting transfers between devices: 25.7 us -> none  [the longest x6 17.2 us: with_halo(): lax.ppermute(lax.slice_in_dim(block, block.shape[dim] - width, None, axis...]
    ppermute x12 -> x0, waiting for transfers between devices: 13.8 us -> none  [the longest x6 12 us: with_halo(): lax.ppermute(lax.slice_in_dim(block, block.shape[dim] - width, None, axis...]
    dot_general x3 -> x0, other arithmetic: 6.23 us -> none  [sweep(): jnp.einsum('nvwxyz,nwxyz->nvxyz', blocks, current, precision=lax.Precisio...]
    sub x6 -> x0, other arithmetic: 5.38 us -> none  [the longest x3 5.16 us: sweep(): resid = right_side - diagonal_part - beside - spectral]
    unnamed x136 -> x10, local copies, waits for them, and re-layouts: 2.06 us -> 5.55 us
    concatenate x5 -> x0, other arithmetic: 2.6 us -> none  [with_halo(): block = jnp.concatenate([low, block, high], axis=dim)]
  transfers between devices with their start and end apart: 15 -> 0, of which waited for: 9 -> 0; matrix products, arithmetic and copies ran while one was open for 33% -> 0% of each run, Pallas kernels for 0% -> 0%
where the time goes in v1:
time: 40.2 us; the launch traced here: 39.9 us
  Pallas kernels  33.1 us (82%)
  local copies, waits for them, and re-layouts  5.55 us (14%)
  between operations  1.3 us (3%)
    pallas_call x1, Pallas kernels, shards(): pl.pallas_call(functools.partial(kernel, ranks, count_x, count_y), out_sh...  33.1 us
    unnamed x10, local copies, waits for them, and re-layouts  5.55 us

profile of v1, /device:TPU:0, one launch (start us, length us, event | category | flops | bytes accessed | tf_op | source)
XLA Modules:
  0.0 39.9 jit_solution(17444905324316041907)
XLA Ops:
  1.3 0.0 copy-start
  1.3 1.4 %copy-done = f32[2,5,5,8,8,128]{5,4,3,2,1,0:T(8,128)S(1)} copy-done((f32[2,5,5,8,8,128]{5,4,3,2,1,0:T(8,128)S(1)}, f32[2,5,5,8,8,128]{5,4,3,2,1,0:T(8,128)}, u32[]{:S(2)}) %copy-start) | copy-done | bytes 1638424
  2.7 0.0 copy-start.1
  2.7 1.0 %copy-done.1 = f32[2,5,8,8,128]{4,3,2,1,0:T(8,128)S(1)} copy-done((f32[2,5,8,8,128]{4,3,2,1,0:T(8,128)S(1)}, f32[2,5,8,8,128]{4,3,2,1,0:T(8,128)}, u32[]{:S(2)}) %copy-start.1) | copy-done | bytes 327704
  3.7 0.0 copy-start.2
  3.7 1.0 %copy-done.2 = f32[2,5,8,8,128]{4,3,2,1,0:T(8,128)S(1)} copy-done((f32[2,5,8,8,128]{4,3,2,1,0:T(8,128)S(1)}, f32[2,5,8,8,128]{4,3,2,1,0:T(8,128)}, u32[]{:S(2)}) %copy-start.2) | copy-done | bytes 327704
  4.7 0.0 copy-start.3
  4.7 0.7 %copy-done.3 = f32[6,5,5]{2,0,1:T(8,128)S(1)} copy-done((f32[6,5,5]{2,0,1:T(8,128)S(1)}, f32[6,5,5]{2,0,1:T(8,128)}, u32[]{:S(2)}) %copy-start.3) | copy-done | bytes 624
  5.4 33.1 %smooth.1 = (f32[2,5,8,8,128]{4,3,2,1,0:T(8,128)S(1)}, f32[2,5,8,8,128]{4,3,2,1,0:T(8,128)S(1)}) custom-call(f32[2,5,8,8,128]{4,3,2,1,0:T(8,128)S(1)} %copy-done.1, f32[2,5,8,8,128]{4,3,2,1,0:T(8,128)S(1)} %copy-done.2, f32[2,5,5,8,8,128]{5,4,3,2,1,0:T(8,128)S(1)} %copy-done, f32[5,6,5]{2,1,0:T(8,128)S(1)} %bitcast.1, f32[1]{0:T(128)S(6)} %copy.9.omega), custom_call_target="tpu_custom_call" | custom-call | tf_op jit(solution)/shard_map/smooth/pallas_call | solution.py:375
  38.5 0.7 %copy.10 = f32[2,5,8,8,128]{4,3,2,1,0:T(8,128)} copy(f32[2,5,8,8,128]{4,3,2,1,0:T(8,128)S(1)} %get-tuple-element.4) | data formatting | bytes 655360
  39.2 0.7 %copy.11 = f32[2,5,8,8,128]{4,3,2,1,0:T(8,128)} copy(f32[2,5,8,8,128]{4,3,2,1,0:T(8,128)S(1)} %get-tuple-element.5) | data formatting | bytes 655360
Async XLA Ops:
  1.3 1.4 %copy-start = (f32[2,5,5,8,8,128]{5,4,3,2,1,0:T(8,128)S(1)}, f32[2,5,5,8,8,128]{5,4,3,2,1,0:T(8,128)}, u32[]{:S(2)}) copy-start(f32[2,5,5,8,8,128]{5,4,3,2,1,0:T(8,128)} %jacobian.1) | copy-start | bytes 4915204
  2.7 1.0 %copy-start.1 = (f32[2,5,8,8,128]{4,3,2,1,0:T(8,128)S(1)}, f32[2,5,8,8,128]{4,3,2,1,0:T(8,128)}, u32[]{:S(2)}) copy-start(f32[2,5,8,8,128]{4,3,2,1,0:T(8,128)} %state.1) | copy-start | bytes 983044
  3.7 1.0 %copy-start.2 = (f32[2,5,8,8,128]{4,3,2,1,0:T(8,128)S(1)}, f32[2,5,8,8,128]{4,3,2,1,0:T(8,128)}, u32[]{:S(2)}) copy-start(f32[2,5,8,8,128]{4,3,2,1,0:T(8,128)} %source.1) | copy-start | bytes 983044
  4.7 0.7 %copy-start.3 = (f32[6,5,5]{2,0,1:T(8,128)S(1)}, f32[6,5,5]{2,0,1:T(8,128)}, u32[]{:S(2)}) copy-start(f32[6,5,5]{2,0,1:T(8,128)} %param.8) | copy-start | bytes 1804

commit v2 on v1

--- a/solution.py
+++ b/solution.py
@@ -9,6 +9,7 @@
 from jax.sharding import PartitionSpec as P
 
 ITERS = 3
+LAG = 2
 MESH = pl.DeviceIdType.MESH
 
 
@@ -245,6 +246,7 @@
     first_row, final_row = row_at == 0, row_at == rows - 1
     first_lane, final_lane = lane_at == 0, lane_at == depth - 1
     speed = omega[0]
+    lag = min(LAG, planes)
 
     def right_side(k, x, n):
         result = []
@@ -327,15 +329,15 @@
                 send_planes(k + 1, x)
                 start_edges(k + 1, x)
 
-                @pl.when(step > 0)
+                @pl.when(step >= lag)
                 def _():
-                    send_parts(k + 1, plane_of(step - 1))
+                    send_parts(k + 1, plane_of(step - lag))
 
             if k > 0:
 
-                @pl.when(step == 0)
+                @pl.when(step < lag)
                 def _():
-                    send_parts(k, plane_of(planes - 1))
+                    send_parts(k, plane_of(planes - lag + step))
 
     @pl.loop(0, planes)
     def _(x):
@@ -388,7 +390,7 @@
                 dma((2, ITERS)), dma((2, ITERS)), dma((2, planes)),
             ],
             compiler_params=pltpu.CompilerParams(
-                collective_id=0, has_side_effects=True, vmem_limit_bytes=48 * 2**20),
+                collective_id=0, has_side_effects=True, vmem_limit_bytes=60 * 1024 * 1024),
             name="smooth",
         )(state, source, jacobian, couplings.transpose(1, 0, 2), omega))
 

time: 40.2 us -> 38.5 us (0.958)
  local copies, waits for them, and re-layouts: 5.55 us -> 3.44 us
    unnamed x10 -> x2, local copies, waits for them, and re-layouts: 5.55 us -> 3.44 us
where the time goes in v2:
time: 38.5 us; the launch traced here: 38.2 us
  Pallas kernels  33.5 us (87%)
  local copies, waits for them, and re-layouts  3.44 us (9%)
  between operations  1.29 us (3%)
    pallas_call x1, Pallas kernels, shards(): pl.pallas_call(functools.partial(kernel, ranks, count_x, count_y), out_sh...  33.5 us
    unnamed x2, local copies, waits for them, and re-layouts  3.44 us

profile of v2, /device:TPU:0, one launch (start us, length us, event | category | flops | bytes accessed | tf_op | source)
XLA Modules:
  0.0 38.2 jit_solution(12730048256253390335)
XLA Ops:
  1.3 33.5 %smooth.1 = (f32[2,5,8,8,128]{4,3,2,1,0:T(8,128)}, f32[2,5,8,8,128]{4,3,2,1,0:T(8,128)}) custom-call(f32[2,5,8,8,128]{4,3,2,1,0:T(8,128)} %state.1, f32[2,5,8,8,128]{4,3,2,1,0:T(8,128)} %source.1, f32[2,5,5,8,8,128]{5,4,3,2,1,0:T(8,128)} %jacobian.1, f32[5,6,5]{2,1,0:T(8,128)} %bitcast.1, f32[1]{0:T(128)S(6)} %copy.9.omega), custom_call_target="tpu_custom_call" | custom-call | tf_op jit(solution)/shard_map/smooth/pallas_call | solution.py:377
  34.8 1.7 %copy.10 = f32[2,5,8,8,128]{4,3,2,1,0:T(8,128)} copy(f32[2,5,8,8,128]{4,3,2,1,0:T(8,128)} %get-tuple-element.4) | data formatting | bytes 655360
  36.5 1.7 %copy.11 = f32[2,5,8,8,128]{4,3,2,1,0:T(8,128)} copy(f32[2,5,8,8,128]{4,3,2,1,0:T(8,128)} %get-tuple-element.5) | data formatting | bytes 655360
